TPU v7x, 768 devices: a whole 4x8x12 slice. The times are simulated.
768 devices in a mesh: blk: 64 (over x, y, core), sub: 12 (over z).
Axes of the slice: x: 4, y: 8, z: 12, core: 2. Of those that a mesh axis runs over, the one named last changes fastest.
Arguments:
- flow_state: float32 [6, 512, 8, 1536], P(None, 'blk', None, 'sub'), may hold values from -6 to 6
- timestep: float32 [512, 8, 1536], P('blk', None, 'sub'), may hold values from 0.05 to 0.3
- coupling: float32 [3, 6, 6], replicated, may hold values from -2.5 to 2.5
- face_type: int32 [64, 2], P('blk'), may hold values from 0 to 3
- face_rot: int32 [64, 2], P('blk'), may hold values from 0 to 3
Outputs:
- updated: float32 [6, 512, 8, 1536], P(None, 'blk', None, 'sub')
- fine_residual: float32 [6, 512, 8, 1536], P(None, 'blk', None, 'sub')
All inputs are finite; a program needn't handle non-finite values.
Results may differ from a plain program's by a relative error of at most 0.0003.
Values sent between devices are 32-bit elements; how exact they have to be, the bound alone decides.
No kernel may reach another device: no remote copies, remote signals or barrier semaphores. Data moves between devices by JAX's collectives and lax.ppermute only.
A program may use at most 64 MiB of HBM per device.

v0:
```python
import jax
import jax.numpy as jnp
from jax import lax
from jax.experimental import pallas as pl
from jax.experimental.pallas import tpu as pltpu
from jax.sharding import PartitionSpec as P


NV = 6
NI = 8
HALO = 10
SEG = 32
VMEM_LIMIT = 12 * 1024 * 1024

C0, C1, C2 = 0.44, -0.26, 0.04


def iota_j():
    return lax.broadcasted_iota(jnp.int32, (8, 128), 0)


def iota_k():
    return lax.broadcasted_iota(jnp.int32, (8, 128), 1)


def rotl(x, shift):
    return pltpu.roll(x, shift % 128, 1)


def rots(x, shift):
    return pltpu.roll(x, shift % 8, 0)


def reverse_j(x):
    j = iota_j()
    x = rots(x, 4)
    x = jnp.where((j // 2) % 2 == 0, rots(x, -2), rots(x, 2))
    return jnp.where(j % 2 == 0, rots(x, -1), rots(x, 1))


def ghost_rows(own2, prev2, next2, kind, flip, turn):
    nearest = []
    for r in range(2):
        picked = []
        for v in range(NV):
            wall = -own2[r][v] if v == 1 else own2[r][v]
            x = jnp.where(kind == 2, wall, 0.0)
            x = jnp.where(kind == 1, next2[r][v], x)
            x = jnp.where(kind == 0, prev2[r][v], x)
            picked.append(jnp.where(flip == 1, reverse_j(x), x))
        a, b = picked[2], picked[3]
        picked[2], picked[3] = jnp.where(turn == 1, -b, a), jnp.where(turn == 1, a, b)
        nearest.append(picked)
    return nearest


def low_ghosts(rows, below, above, meta):
    lo = ghost_rows([rows[0], rows[1]], [below[1], below[0]], [above[0], above[1]], *meta[:3])
    return [lo[1], lo[0]]


def high_ghosts(rows, below, above, meta):
    return ghost_rows([rows[-1], rows[-2]], [above[0], above[1]], [below[1], below[0]], *meta[3:])


def with_ghosts(rows, below, above, meta):
    return low_ghosts(rows, below, above, meta) + rows + high_ghosts(rows, below, above, meta)


def flux(q, a, d):
    half = 0.5 * q[1 + d]
    out = []
    for u in range(NV):
        acc = (a(d, u, u) + half) * q[u]
        for v in range(NV):
            if v != u:
                acc = acc + a(d, u, v) * q[v]
        out.append(acc)
    return out


def flux_j(q, a):
    out, mirrored = [], []
    for u in range(NV):
        even = None
        for v in range(NV):
            if v != 2:
                term = a(1, u, v) * q[v]
                even = term if even is None else even + term
        if u == 2:
            even = even + 0.5 * (q[2] * q[2])
            odd = a(1, 2, 2) * q[2]
        else:
            odd = q[2] * (a(1, u, 2) + 0.5 * q[u])
        out.append(even + odd)
        mirrored.append(even - odd)
    return out, mirrored


def j_weights(unit):
    j = iota_j() // unit
    n = 8 // unit
    out = []
    for sign in (1.0, -1.0):
        end = (j == 0) | (j == n - 1)
        centre = jnp.where(end, C0 + sign * C1, C0) + 2 * C0
        near = C1 + sign * C2
        below = jnp.where(j == 0, 0.0, jnp.where((j == 1) | (j == n - 1), near, C1))
        above = jnp.where(j == n - 1, 0.0, jnp.where((j == 0) | (j == n - 2), near, C1))
        if n == 4:
            two = None
        else:
            two = (jnp.where(j >= 2, C2, 0.0), jnp.where(j <= n - 3, C2, 0.0))
        out.append((centre, below, above, two))
    return out


def seg():
    return iota_k() // SEG


def place():
    return iota_k() % SEG


def second_index(fj, gj, q, u, unit, weights, ends):
    centre, below, above, two = weights[1 if u == 2 else 0]
    x = q[u]
    acc = centre * x + below * rots(x, unit) + above * rots(x, -unit)
    if two is None:
        acc = acc + C2 * rots(x, 4)
    else:
        acc = acc + two[0] * rots(x, 2) + two[1] * rots(x, -2)
    up = jnp.where(ends[1], gj[u], rots(fj[u], -unit))
    down = jnp.where(ends[0], gj[u], rots(fj[u], unit))
    return acc + (up - down)


def residual2(padded, halo, a, unit, start=0):
    n = len(padded) - 4
    k, j = iota_k(), iota_j()
    weights = j_weights(unit)
    ends = (j < unit, j >= 8 - unit)
    low1, low2 = k < unit, k < 2 * unit
    high1, high2 = k >= 128 - unit, k >= 128 - 2 * unit
    upper = place() >= HALO
    edge = []
    for tile in halo or ():
        f = flux(tile, a, 2)
        edge.append([jnp.where(upper, f[u] + C1 * tile[u], f[u] - C1 * tile[u]) for u in range(NV)])
    beside = []
    for i in range(n if halo else 0):
        g, first = unit * (start + i) // 4, unit * (start + i) % 4 * SEG + HALO
        beside.append([(rotl(halo[g][u], -first), rotl(edge[g][u], -first)) for u in range(NV)])
    fi = {m: flux(padded[m], a, 0) for m in range(1, n + 3)}
    result = []
    for i in range(n):
        m = i + 2
        q = padded[m]
        fj, gj = flux_j(q, a)
        fk = flux(q, a, 2)
        row = []
        for u in range(NV):
            x = q[u]
            s, e = beside[i][u] if halo else (0.0, 0.0)
            acc = second_index(fj, gj, q, u, unit, weights, ends)
            acc = acc + (fi[m + 1][u] - fi[m - 1][u])
            acc = acc + C1 * (padded[m + 1][u] + padded[m - 1][u]) + C2 * (padded[m + 2][u] + padded[m - 2][u])
            t = C1 * x
            acc = acc + rotl(jnp.where(low1, e, fk[u] + t), -unit)
            acc = acc - rotl(jnp.where(high1, e, fk[u] - t), unit)
            acc = acc + C2 * (rotl(jnp.where(low2, s, x), -2 * unit) + rotl(jnp.where(high2, s, x), 2 * unit))
            row.append(acc)
        result.append(row)
    return result


def halo_residual2(halo, ghost, own, a):
    r, o = seg(), place()
    j = iota_j()
    weights = j_weights(1)
    ends = (j < 1, j >= 7)
    first, last, low, high = r == 0, r == 3, r < 2, r >= 2
    tiles = [halo[0], halo[1], ghost]
    up_i, down_i = [], []
    for t in tiles:
        f = flux(t, a, 0)
        up_i.append([f[u] + C1 * t[u] for u in range(NV)])
        down_i.append([f[u] - C1 * t[u] for u in range(NV)])
    upper = o >= HALO
    after1, after2 = o == HALO, (o == HALO) | (o == HALO + 1)
    before1, before2 = o == HALO - 1, (o == HALO - 1) | (o == HALO - 2)
    result = []
    for g in range(2):
        q, nxt, prv = tiles[g], (g + 1) % 3, (g + 2) % 3
        fj, gj = flux_j(q, a)
        fk = flux(q, a, 2)
        fo = flux(own[g], a, 2)
        row = []
        for u in range(NV):
            x, y = q[u], own[g][u]
            acc = second_index(fj, gj, q, u, 1, weights, ends)
            acc = acc + rotl(jnp.where(first, up_i[nxt][u], up_i[g][u]), -SEG)
            acc = acc - rotl(jnp.where(last, down_i[prv][u], down_i[g][u]), SEG)
            acc = acc + C2 * rotl(jnp.where(low, tiles[nxt][u], x) + jnp.where(high, tiles[prv][u], x), 2 * SEG)
            t = C1 * x
            e = jnp.where(upper, fo[u] + C1 * y, fo[u] - C1 * y)
            acc = acc + rotl(jnp.where(after1, e, fk[u] + t), -1)
            acc = acc - rotl(jnp.where(before1, e, fk[u] - t), 1)
            acc = acc + C2 * (rotl(jnp.where(after2, y, x), -2) + rotl(jnp.where(before2, y, x), 2))
            row.append(acc)
        result.append(row)
    return result


def pack_ends(rows):
    r = seg()
    out = []
    for g in range(2):
        tile = []
        for v in range(NV):
            acc = rotl(rows[4 * g][v], HALO)
            for p in range(1, 4):
                acc = jnp.where(r == p, rotl(rows[4 * g + p][v], HALO + p * SEG), acc)
            tile.append(acc)
        out.append(tile)
    return out


def halo_ghost(halo, below, above, meta):
    t_lo, flip_lo, turn_lo, t_hi, flip_hi, turn_hi = meta
    r = seg()
    high_side = r < 2
    even_part = r % 2 == 0

    def turned(x):
        return jnp.where(even_part, rotl(x, SEG), rotl(x, -SEG))

    flip = jnp.where(high_side, flip_hi, flip_lo)
    picked = []
    for v in range(NV):
        wall_lo, wall_hi = turned(halo[0][v]), turned(halo[1][v])
        if v == 1:
            wall_lo, wall_hi = -wall_lo, -wall_hi
        hi = jnp.where(t_hi == 2, wall_hi, 0.0)
        hi = jnp.where(t_hi == 1, turned(below[v]), hi)
        hi = jnp.where(t_hi == 0, above[v], hi)
        lo = jnp.where(t_lo == 2, wall_lo, 0.0)
        lo = jnp.where(t_lo == 1, turned(above[v]), lo)
        lo = jnp.where(t_lo == 0, below[v], lo)
        x = jnp.where(high_side, hi, lo)
        picked.append(jnp.where(flip == 1, reverse_j(x), x))
    turn = jnp.where(high_side, turn_hi, turn_lo) == 1
    b, c = picked[2], picked[3]
    picked[2], picked[3] = jnp.where(turn, -c, b), jnp.where(turn, b, c)
    return picked


def cell_mean(x):
    x = x + jnp.where(iota_j() % 2 == 0, rots(x, -1), rots(x, 1))
    x = x + jnp.where(iota_k() % 2 == 0, rotl(x, -1), rotl(x, 1))
    return 0.125 * x


def restrict_rows(rows):
    return [[cell_mean(rows[2 * c][v] + rows[2 * c + 1][v]) for v in range(len(rows[0]))] for c in range(len(rows) // 2)]


def halo_means(tiles):
    even = seg() % 2 == 0
    tiles = [x + jnp.where(even, rotl(x, -SEG), rotl(x, SEG)) for x in tiles]
    return [cell_mean(x) for x in tiles]


def load(ref, first, count):
    return [[ref[v, first + r] for v in range(NV)] for r in range(count)]


def store(ref, first, rows):
    for r, row in enumerate(rows):
        for v in range(NV):
            ref[v, first + r] = row[v]


def load_tiles(ref):
    return [[ref[g, v] for v in range(NV)] for g in range(2)]


def store_tiles(ref, tiles):
    for g in range(2):
        for v in range(NV):
            ref[g, v] = tiles[g][v]


def table_kernel(a_ref, type_ref, rot_ref, table_ref):
    values = [a_ref[d, u, v] for d in range(3) for u in range(NV) for v in range(NV)]
    for face in range(2):
        kind, rot = type_ref[0, face], rot_ref[0, face]
        values += [kind.astype(jnp.float32), (rot % 2).astype(jnp.float32), (rot // 2 % 2).astype(jnp.float32)]
    for n, value in enumerate(values):
        table_ref[n] = jnp.full((8, 128), value, jnp.float32)


def coefficients(table_ref):
    return lambda d, u, v: table_ref[(d * NV + u) * NV + v]


def meta_of(table_ref):
    first = 3 * NV * NV
    return [table_ref[first + n] for n in range(6)]


def masked(tiles):
    o = place()
    s = lax.axis_index("sub")
    final = lax.axis_size("sub") - 1
    inside = ((o < HALO) & (s != 0)) | ((o >= HALO) & (o < 2 * HALO) & (s != final))
    return [[jnp.where(inside, x, 0.0) for x in tile] for tile in tiles]


def is_even():
    return lax.axis_index("blk") % 2 == 0


def send(ma, mb, at, first, last):
    even = is_even()
    for n, (lo, hi) in enumerate(zip(first, last)):
        ma[at + n] = jnp.where(even, hi, lo)
        mb[at + n] = jnp.where(even, lo, hi)


def put(ref, at, tiles):
    for n, x in enumerate(tiles):
        ref[at + n] = x


def receive(ga, gb, at, count):
    even = is_even()
    below, above = [], []
    for n in range(at, at + count):
        a, b = ga[n], gb[n]
        below.append(jnp.where(even, b, a))
        above.append(jnp.where(even, a, b))
    return below, above


def send_rows(ma, mb, at, rows):
    send(ma, mb, at, rows[0] + rows[1], rows[-2] + rows[-1])


def receive_rows(ga, gb, at):
    below, above = receive(ga, gb, at, 2 * NV)
    return [below[:NV], below[NV:]], [above[:NV], above[NV:]]


def halo_first(halo):
    low = seg() < 2
    return [jnp.where(low, halo[0][p], rotl(halo[0][p + 1], 64)) for p in range(0, NV, 2)]


def halo_last(halo):
    low = seg() < 2
    return [jnp.where(low, rotl(halo[1][p + 1], 64), halo[1][p]) for p in range(0, NV, 2)]


def send_halo(ma, mb, at, halo):
    send(ma, mb, at, halo_first(halo), halo_last(halo))


def receive_halo(ga, gb, at):
    below, above = receive(ga, gb, at, NV // 2)

    def spread(tiles):
        return [y for x in tiles for y in (x, rotl(x, 64))]

    return spread(below), spread(above)


def joined(first, second):
    j_even, k_even = iota_j() % 2 == 0, iota_k() % 2 == 0
    out = []
    for v in range(NV):
        x, y = (jnp.where(j_even, first[r][v], second[r][v]) for r in range(2))
        out.append(jnp.where(k_even, x, y))
    return out


def receive_coarse(ga, gb, at):
    j_even, k_even = iota_j() % 2 == 0, iota_k() % 2 == 0
    fields = ([], [])
    for tiles in receive(ga, gb, at, NV):
        rows = ([], [])
        for x in tiles:
            rows[0].append(jnp.where(k_even, x, rotl(x, 1)))
            rows[1].append(jnp.where(k_even, rotl(x, -1), x))
        fields[0].append([[jnp.where(j_even, x, rots(x, 1)) for x in row] for row in rows])
        fields[1].append([[jnp.where(j_even, rots(x, -1), x) for x in row] for row in rows])
    return fields


def prime_kernel(out_ref):
    out_ref[...] = jnp.zeros_like(out_ref)


def pack_kernel(prime_ref, q_ref, dt_ref, ends_ref, ma, mb, to_left, to_right):
    rows = load(q_ref, 0, NI)
    ends = pack_ends(rows)
    store_tiles(ends_ref, ends)
    r, lower = seg(), place() < HALO
    tiles = ends[0] + ends[1]
    for g in range(2):
        acc = rotl(dt_ref[4 * g], HALO)
        for p in range(1, 4):
            acc = jnp.where(r == p, rotl(dt_ref[4 * g + p], HALO + p * SEG), acc)
        tiles.append(acc)
    for n in range(NV + 1):
        x, y = tiles[2 * n], tiles[2 * n + 1]
        to_right[n] = jnp.where(lower, x, rotl(y, HALO))
        to_left[n] = jnp.where(lower, rotl(y, -HALO), x)
    send_rows(ma, mb, 0, rows)


def unpack(from_right, from_left):
    lower = place() < HALO
    tiles = []
    for n in range(NV + 1):
        x, y = from_left[n], from_right[n]
        tiles.append(jnp.where(lower, x, y))
        tiles.append(jnp.where(lower, rotl(x, -HALO), rotl(y, HALO)))
    halo = masked([tiles[:NV], tiles[NV : 2 * NV]])
    return halo, tiles[2 * NV :]


def advance(start, dt, twice, factor):
    return [[start[i][v] - (0.5 * factor * dt[i]) * twice[i][v] for v in range(NV)] for i in range(len(start))]


def end_rows(start, rows, halo, dt_ref, ga, gb, a, meta, factor):
    below, above = receive_rows(ga, gb, 0)
    dt = [dt_ref[i] for i in range(NI)]
    low = low_ghosts(rows, below, above, meta) + rows[:4]
    high = rows[-4:] + high_ghosts(rows, below, above, meta)
    first = advance(start[:2], dt[:2], residual2(low, halo, a, 1), factor)
    last = advance(start[-2:], dt[-2:], residual2(high, halo, a, 1, NI - 2), factor)
    return first + last


def first_ends_kernel(table_ref, q_ref, dt_ref, ga, gb, from_right, from_left, h0_ref, dth_ref, ma, mb):
    a, meta = coefficients(table_ref), meta_of(table_ref)
    h0, dth = unpack(from_right, from_left)
    store_tiles(h0_ref, h0)
    put(dth_ref, 0, dth)
    send_halo(ma, mb, 2 * NV, h0)
    rows = load(q_ref, 0, NI)
    send_rows(ma, mb, 0, end_rows(rows, rows, h0, dt_ref, ga, gb, a, meta, 0.4))


def first_kernel(table_ref, q_ref, dt_ref, ga, gb, h0_ref, t1_ref):
    a, meta = coefficients(table_ref), meta_of(table_ref)
    t0 = load(q_ref, 0, NI)
    below, above = receive_rows(ga, gb, 0)
    twice = residual2(with_ghosts(t0, below, above, meta), load_tiles(h0_ref), a, 1)
    store(t1_ref, 0, advance(t0, [dt_ref[i] for i in range(NI)], twice, 0.4))


def second_ends_kernel(table_ref, q_ref, t1_ref, h0_ref, ends_ref, dt_ref, dth_ref, ga, gb, h1_ref, ma, mb):
    a, meta = coefficients(table_ref), meta_of(table_ref)
    h0 = load_tiles(h0_ref)
    below, above = receive_halo(ga, gb, 2 * NV)
    twice = halo_residual2(h0, halo_ghost(h0, below, above, meta), load_tiles(ends_ref), a)
    h1 = masked(advance(h0, [dth_ref[g] for g in range(2)], twice, 0.4))
    store_tiles(h1_ref, h1)
    send_halo(ma, mb, 2 * NV, h1)
    t0, t1 = load(q_ref, 0, NI), load(t1_ref, 0, NI)
    send_rows(ma, mb, 0, end_rows(t0, t1, h1, dt_ref, ga, gb, a, meta, 1.0))


def second_kernel(table_ref, q_ref, t1_ref, h1_ref, dt_ref, ga, gb, t2_ref):
    a, meta = coefficients(table_ref), meta_of(table_ref)
    t0, t1 = load(q_ref, 0, NI), load(t1_ref, 0, NI)
    below, above = receive_rows(ga, gb, 0)
    twice = residual2(with_ghosts(t1, below, above, meta), load_tiles(h1_ref), a, 1)
    store(t2_ref, 0, advance(t0, [dt_ref[i] for i in range(NI)], twice, 1.0))


def first_section(rows, res, dt):
    start, mean = restrict_rows(rows), restrict_rows(res)
    c1 = []
    for c in range(len(start)):
        step = cell_mean(dt[2 * c] + dt[2 * c + 1])
        c1.append([start[c][v] - (0.4 * step) * mean[c][v] for v in range(NV)])
    return start, mean, c1


def third_kernel(
    table_ref, t1_ref, t2_ref, h0_ref, h1_ref, dt_ref, dth_ref, ga, gb, res_ref, h2_ref, start_ref, c1_ref, mean_ref, ma, mb
):
    a, meta = coefficients(table_ref), meta_of(table_ref)
    h0, h1 = load_tiles(h0_ref), load_tiles(h1_ref)
    below, above = receive_halo(ga, gb, 2 * NV)
    twice = halo_residual2(h1, halo_ghost(h1, below, above, meta), pack_ends(load(t1_ref, 0, NI)), a)
    h2 = masked(advance(h0, [dth_ref[g] for g in range(2)], twice, 1.0))
    store_tiles(h2_ref, h2)
    send_halo(ma, mb, NV, h2)
    t2 = load(t2_ref, 0, NI)
    below, above = receive_rows(ga, gb, 0)
    twice = residual2(with_ghosts(t2, below, above, meta), h2, a, 1)
    res = [[0.5 * x for x in row] for row in twice]
    store(res_ref, 0, res)
    start, mean, c1 = first_section(t2, res, [dt_ref[i] for i in range(NI)])
    store(start_ref, 0, start)
    store(mean_ref, 0, mean)
    store(c1_ref, 0, c1)
    send(ma, mb, 0, joined(c1[:2], start[:2]), joined(c1[2:], start[2:]))


def early_kernel(table_ref, start_ref, c1_ref, h2_ref, part_ref):
    a = coefficients(table_ref)
    half = NI // 2
    h2 = load_tiles(h2_ref)
    start_h = halo_means(h2[0] + h2[1])
    ghost = [[jnp.zeros((8, 128), jnp.float32)] * NV] * 2
    twice0 = residual2(ghost + load(start_ref, 0, half) + ghost, [start_h[:NV], start_h[NV:]], a, 2)
    twice1 = residual2(ghost + load(c1_ref, 0, half) + ghost, None, a, 2)
    store(part_ref, 0, [[twice1[c][v] - twice0[c][v] for v in range(NV)] for c in range(half)])


def halo_part(halo, a):
    o, k = place(), iota_k()
    high1, low1 = (o == HALO - 2) | (o == HALO - 1), (o == HALO) | (o == HALO + 1)
    high2, low2 = (o >= HALO - 4) & (o < HALO), (o >= HALO) & (o < HALO + 4)
    spread = []
    for tile in halo:
        f = flux(tile, a, 2)
        row = []
        for u in range(NV):
            x = tile[u]
            w = jnp.where(high1, rotl(f[u] + C1 * x, -2), 0.0) - jnp.where(low1, rotl(f[u] - C1 * x, 2), 0.0)
            row.append(w + C2 * (jnp.where(high2, rotl(x, -4), 0.0) + jnp.where(low2, rotl(x, 4), 0.0)))
        spread.append(row)
    near = (k < 4) | (k >= 124)
    out = []
    for c in range(NI // 2):
        g, first = 2 * c // 4, 2 * c % 4 * SEG + HALO
        out.append([jnp.where(near, rotl(spread[g][u], -first), 0.0) for u in range(NV)])
    return out


def ghost_part(low, high, a):
    fl, fh = flux(low[1], a, 0), flux(high[0], a, 0)
    rows = ([], [], [], [])
    for u in range(NV):
        rows[0].append(C1 * low[1][u] + C2 * low[0][u] - fl[u])
        rows[1].append(C2 * low[1][u])
        rows[2].append(C2 * high[0][u])
        rows[3].append(C1 * high[0][u] + C2 * high[1][u] + fh[u])
    return rows


def fourth_kernel(
    table_ref, t2_ref, h2_ref, start_ref, c1_ref, mean_ref, part_ref, dt_ref, dth_ref, res_ref, ga, gb, out_hbm, res_hbm, out_ref, sems
):
    a, meta = coefficients(table_ref), meta_of(table_ref)
    half = NI // 2
    copies = [pltpu.make_async_copy(res_ref, res_hbm, sems.at[half])]
    copies[0].start()
    h2, t2 = load_tiles(h2_ref), load(t2_ref, 0, NI)
    below, above = receive_halo(ga, gb, NV)
    twice = halo_residual2(h2, halo_ghost(h2, below, above, meta), pack_ends(t2), a)
    means = halo_means(h2[0] + h2[1] + [dth_ref[0], dth_ref[1]] + twice[0] + twice[1])
    start_h, step_h, mean_h = means[: 2 * NV], means[2 * NV : 2 * NV + 2], means[2 * NV + 2 :]
    c1_h = [start_h[t] - (0.2 * step_h[t // NV]) * mean_h[t] for t in range(2 * NV)]
    halo = halo_part(masked([c1_h[:NV], c1_h[NV:]]), a)
    ghosts = []
    for ref, (below, above) in zip((c1_ref, start_ref), receive_coarse(ga, gb, 0)):
        rows = load(ref, 0, half)
        ghosts.append(ghost_part(low_ghosts(rows, below, above, meta), high_ghosts(rows, below, above, meta), a))
    for c in range(half):
        step = cell_mean(dt_ref[2 * c] + dt_ref[2 * c + 1])
        for v in range(NV):
            twice_change = part_ref[v, c] + (ghosts[0][c][v] - ghosts[1][c][v]) + halo[c][v]
            change = -step * (0.5 * twice_change + mean_ref[v, c])
            out_ref[v, 2 * c] = t2[2 * c][v] + change
            out_ref[v, 2 * c + 1] = t2[2 * c + 1][v] + change
    for c in range(half):
        rows = pl.ds(2 * c, 2)
        copies.append(pltpu.make_async_copy(out_ref.at[:, rows], out_hbm.at[:, rows], sems.at[c]))
        copies[-1].start()
    for copy in copies:
        copy.wait()


def field(rows):
    return (NV, rows, 8, 128)


def tiles_of(*count):
    return (*count, 8, 128)


def call(kernel, arrays, outs, scalars=(), out_space=pltpu.VMEM, scratch=()):
    smem, vmem = pl.BlockSpec(memory_space=pltpu.SMEM), pl.BlockSpec(memory_space=pltpu.VMEM)
    return pl.pallas_call(
        kernel,
        out_shape=[jax.ShapeDtypeStruct(shape, jnp.float32) for shape in outs],
        in_specs=[smem] * len(scalars) + [vmem] * len(arrays),
        out_specs=[pl.BlockSpec(memory_space=out_space)] * len(outs),
        scratch_shapes=scratch,
        compiler_params=pltpu.CompilerParams(vmem_limit_bytes=VMEM_LIMIT),
    )(*scalars, *arrays)


def cycle(flow_state, timestep, coupling, face_type, face_rot):
    blocks, parts = lax.axis_size("blk"), lax.axis_size("sub")
    chip = [(b, b ^ 1) for b in range(blocks)]
    link = [(b, (b + 1) % blocks if b % 2 else (b - 1) % blocks) for b in range(blocks)]
    ahead = [(s, s + 1) for s in range(parts - 1)]
    back = [(s + 1, s) for s in range(parts - 1)]
    pair = tiles_of(2, NV)

    def exchange(ma, mb):
        gb = lax.ppermute(mb, "blk", link)
        ga = lax.ppermute(ma, "blk", chip)
        return ga, gb

    (table,) = call(table_kernel, (), (tiles_of(3 * NV * NV + 6),), (coupling, face_type, face_rot))
    (prime,) = call(prime_kernel, (), (tiles_of(114),))
    ends, ma, mb, to_left, to_right = call(
        pack_kernel,
        (prime, flow_state, timestep),
        (pair, tiles_of(2 * NV), tiles_of(2 * NV), tiles_of(NV + 1), tiles_of(NV + 1)),
    )
    ga, gb = exchange(ma, mb)
    from_right = lax.ppermute(to_left, "sub", back)
    from_left = lax.ppermute(to_right, "sub", ahead)

    message = tiles_of(2 * NV + NV // 2)
    h0, dth, ma, mb = call(
        first_ends_kernel,
        (table, flow_state, timestep, ga, gb, from_right, from_left),
        (pair, tiles_of(2), message, message),
    )
    (t1,) = call(first_kernel, (table, flow_state, timestep, ga, gb, h0), (field(NI),))
    ga, gb = exchange(ma, mb)

    h1, ma, mb = call(
        second_ends_kernel,
        (table, flow_state, t1, h0, ends, timestep, dth, ga, gb),
        (pair, message, message),
    )
    (t2,) = call(second_kernel, (table, flow_state, t1, h1, timestep, ga, gb), (field(NI),))
    ga, gb = exchange(ma, mb)

    message = tiles_of(NV + NV // 2)
    coarse = field(NI // 2)
    res, h2, start, c1, mean, ma, mb = call(
        third_kernel,
        (table, t1, t2, h0, h1, timestep, dth, ga, gb),
        (field(NI), pair, coarse, coarse, coarse, message, message),
    )
    (part,) = call(early_kernel, (table, start, c1, h2), (coarse,))
    ga, gb = exchange(ma, mb)

    updated, res = call(
        fourth_kernel,
        (table, t2, h2, start, c1, mean, part, timestep, dth, res, ga, gb),
        (field(NI), field(NI)),
        out_space=pltpu.HBM,
        scratch=(pltpu.VMEM(field(NI), jnp.float32), pltpu.SemaphoreType.DMA((NI // 2 + 1,))),
    )
    return (updated, res)


def solution(mesh):
    return jax.shard_map(
        cycle,
        mesh=mesh,
        in_specs=(
            P(None, "blk", None, "sub"),
            P("blk", None, "sub"),
            P(),
            P("blk", None),
            P("blk", None),
        ),
        out_specs=(P(None, "blk", None, "sub"), P(None, "blk", None, "sub")),
        check_vma=False,
    )
```

profile of v0, /device:TPU:512, one launch (start us, length us, event | category | flops | bytes accessed | tf_op | source)
XLA Modules:
  0.0 57.8 jit_solution(10452765274817132849)
XLA Ops:
  0.6 0.0 copy-start.1
  0.6 0.0 copy-start
  0.7 0.7 %copy-done.1 = f32[8,8,128]{2,1,0:T(8,128)S(1)} copy-done((f32[8,8,128]{2,1,0:T(8,128)S(1)}, f32[8,8,128]{2,1,0:T(8,128)}, u32[]{:S(2)}) %copy-start.1) | copy-done | bytes 32792
  1.4 0.2 copy-done
  1.6 0.0 copy-start.2
  1.6 0.2 shard_map.70
  1.8 1.9 %collective-permute-start = (f32[12,8,128]{2,1,0:T(8,128)S(1)}, f32[12,8,128]{2,1,0:T(8,128)S(1)}, u32[]{:S(2)}, u32[]{:S(2)}) collective-permute-start(f32[12,8,128]{2,1,0:T(8,128)S(1)} %get-tuple-element.21), channel_id=1, source_target_pairs={{0,12},{12,0},{24,36},{36,24},{48,60},{60,48},{72,84},{84,72},{96,... | collective-permute-start | bytes 147464 | tf_op jit(solution)/shard_map/ppermute | solution.py:623
  3.7 7.7 %collective-permute-start.1 = (f32[12,8,128]{2,1,0:T(8,128)S(1)}, f32[12,8,128]{2,1,0:T(8,128)S(1)}, u32[]{:S(2)}, u32[]{:S(2)}) collective-permute-start(f32[12,8,128]{2,1,0:T(8,128)S(1)} %get-tuple-element.22), channel_id=1, source_target_pairs={{0,756},{12,24},{24,12},{36,48},{48,36},{60,72},{72,60},{84,96},{9... | collective-permute-start | bytes 147464 | tf_op jit(solution)/shard_map/ppermute | solution.py:622
  11.4 0.0 copy-start.3
  11.4 0.0 copy-start.4
  11.4 3.7 %collective-permute-start.2 = (f32[7,8,128]{2,1,0:T(8,128)S(1)}, f32[7,8,128]{2,1,0:T(8,128)S(1)}, u32[]{:S(2)}, u32[]{:S(2)}) collective-permute-start(f32[7,8,128]{2,1,0:T(8,128)S(1)} %get-tuple-element.23), channel_id=1, source_target_pairs={{1,0},{2,1},{3,2},{4,3},{5,4},{6,5},{7,6},{8,7},{9,8},{10,9},{11,1... | collective-permute-start | bytes 86024 | tf_op jit(solution)/shard_map/ppermute | solution.py:634
  15.1 2.2 %collective-permute-start.3 = (f32[7,8,128]{2,1,0:T(8,128)S(1)}, f32[7,8,128]{2,1,0:T(8,128)S(1)}, u32[]{:S(2)}, u32[]{:S(2)}) collective-permute-start(f32[7,8,128]{2,1,0:T(8,128)S(1)} %get-tuple-element.24), channel_id=1, source_target_pairs={{0,1},{1,2},{2,3},{3,4},{4,5},{5,6},{6,7},{7,8},{8,9},{9,10},{10,1... | collective-permute-start | bytes 86024 | tf_op jit(solution)/shard_map/ppermute | solution.py:635
  17.2 0.0 copy-done.2
  17.3 0.0 copy-done.3
  17.3 0.0 copy-done.4
  17.3 0.8 %shard_map.68.table_ref = f32[114,8,128]{2,1,0:T(8,128)S(1)} custom-call(f32[3,6,6]{2,1,0:T(8,128)S(1)} %copy-done.2, s32[1,2]{1,0:T(1,128)S(1)} %copy-done.3, s32[1,2]{1,0:T(1,128)S(1)} %copy-done.4), custom_call_target="tpu_custom_call" | custom-call | tf_op jit(solution)/shard_map/pallas_call | solution.py:603
  18.1 0.0 collective-permute-done.2.from_right
  18.1 3.9 %collective-permute-done.3.from_left = f32[7,8,128]{2,1,0:T(8,128)S(1)} collective-permute-done((f32[7,8,128]{2,1,0:T(8,128)S(1)}, f32[7,8,128]{2,1,0:T(8,128)S(1)}, u32[]{:S(2)}, u32[]{:S(2)}) %collective-permute-start.3) | collective-permute-done | bytes 28704 | tf_op jit(solution)/shard_map/ppermute | solution.py:635
  22.0 0.0 collective-permute-done.ga
  22.0 0.0 collective-permute-done.1.gb
  22.1 0.5 shard_map.71
  22.5 1.9 %collective-permute-start.4 = (f32[15,8,128]{2,1,0:T(8,128)S(1)}, f32[15,8,128]{2,1,0:T(8,128)S(1)}, u32[]{:S(2)}, u32[]{:S(2)}) collective-permute-start(f32[15,8,128]{2,1,0:T(8,128)S(1)} %get-tuple-element.28), channel_id=1, source_target_pairs={{0,12},{12,0},{24,36},{36,24},{48,60},{60,48},{72,84},{84,72},{96,... | collective-permute-start | bytes 184328 | tf_op jit(solution)/shard_map/ppermute | solution.py:623
  24.5 3.4 %collective-permute-start.5 = (f32[15,8,128]{2,1,0:T(8,128)S(1)}, f32[15,8,128]{2,1,0:T(8,128)S(1)}, u32[]{:S(2)}, u32[]{:S(2)}) collective-permute-start(f32[15,8,128]{2,1,0:T(8,128)S(1)} %get-tuple-element.29), channel_id=1, source_target_pairs={{0,756},{12,24},{24,12},{36,48},{48,36},{60,72},{72,60},{84,96},{9... | collective-permute-start | bytes 184328 | tf_op jit(solution)/shard_map/ppermute | solution.py:622
  27.8 0.7 %shard_map.72.t1_ref = f32[6,8,8,128]{3,2,1,0:T(8,128)S(1)} custom-call(f32[114,8,128]{2,1,0:T(8,128)S(1)} %shard_map.68.table_ref, f32[6,8,8,128]{3,2,1,0:T(8,128)S(1)} %copy-done, f32[8,8,128]{2,1,0:T(8,128)S(1)} %copy-done.1, f32[12,8,128]{2,1,0:T(8,128)S(1)} %collective-permute-done.ga, f32[12,8,128]{2,1,0:T(8,128)S(1)} %collective-permute-done.1.gb, ...), custom_call_target="tpu_custom_call" | custom-call | tf_op jit(solution)/shard_map/pallas_call | solution.py:603
  28.5 0.0 collective-permute-done.4.ga
  28.5 4.8 %collective-permute-done.5.gb = f32[15,8,128]{2,1,0:T(8,128)S(1)} collective-permute-done((f32[15,8,128]{2,1,0:T(8,128)S(1)}, f32[15,8,128]{2,1,0:T(8,128)S(1)}, u32[]{:S(2)}, u32[]{:S(2)}) %collective-permute-start.5) | collective-permute-done | bytes 61472 | tf_op jit(solution)/shard_map/ppermute | solution.py:622
  33.3 0.7 %shard_map.73 = (f32[2,6,8,128]{3,2,1,0:T(8,128)S(1)}, f32[15,8,128]{2,1,0:T(8,128)S(1)}, f32[15,8,128]{2,1,0:T(8,128)S(1)}) custom-call(f32[114,8,128]{2,1,0:T(8,128)S(1)} %shard_map.68.table_ref, f32[6,8,8,128]{3,2,1,0:T(8,128)S(1)} %copy-done, f32[6,8,8,128]{3,2,1,0:T(8,128)S(1)} %shard_map.72.t1_ref, f32[2,6,8,128]{3,2,1,0:T(8,128)S(1)} %get-tuple-element.25.h0_ref, ...), custom_call_target="tpu_custom_call" | custom-call | tf_op jit(solution)/shard_map/pallas_call | solution.py:603
  34.0 1.9 %collective-permute-start.6 = (f32[15,8,128]{2,1,0:T(8,128)S(1)}, f32[15,8,128]{2,1,0:T(8,128)S(1)}, u32[]{:S(2)}, u32[]{:S(2)}) collective-permute-start(f32[15,8,128]{2,1,0:T(8,128)S(1)} %get-tuple-element.31), channel_id=1, source_target_pairs={{0,12},{12,0},{24,36},{36,24},{48,60},{60,48},{72,84},{84,72},{96,... | collective-permute-start | bytes 184328 | tf_op jit(solution)/shard_map/ppermute | solution.py:623
  35.9 3.4 %collective-permute-start.7 = (f32[15,8,128]{2,1,0:T(8,128)S(1)}, f32[15,8,128]{2,1,0:T(8,128)S(1)}, u32[]{:S(2)}, u32[]{:S(2)}) collective-permute-start(f32[15,8,128]{2,1,0:T(8,128)S(1)} %get-tuple-element.32), channel_id=1, source_target_pairs={{0,756},{12,24},{24,12},{36,48},{48,36},{60,72},{72,60},{84,96},{9... | collective-permute-start | bytes 184328 | tf_op jit(solution)/shard_map/ppermute | solution.py:622
  39.3 0.7 %shard_map.74.t2_ref = f32[6,8,8,128]{3,2,1,0:T(8,128)S(1)} custom-call(f32[114,8,128]{2,1,0:T(8,128)S(1)} %shard_map.68.table_ref, f32[6,8,8,128]{3,2,1,0:T(8,128)S(1)} %copy-done, f32[6,8,8,128]{3,2,1,0:T(8,128)S(1)} %shard_map.72.t1_ref, f32[2,6,8,128]{3,2,1,0:T(8,128)S(1)} %get-tuple-element.30.h1_ref, f32[8,8,128]{2,1,0:T(8,128)S(1)} %copy-done.1, ...), custom_call_target="tpu_custom_call" | custom-call | tf_op jit(solution)/shard_map/pallas_call | solution.py:603
  40.0 0.0 collective-permute-done.6.ga
  40.0 4.8 %collective-permute-done.7.gb = f32[15,8,128]{2,1,0:T(8,128)S(1)} collective-permute-done((f32[15,8,128]{2,1,0:T(8,128)S(1)}, f32[15,8,128]{2,1,0:T(8,128)S(1)}, u32[]{:S(2)}, u32[]{:S(2)}) %collective-permute-start.7) | collective-permute-done | bytes 61472 | tf_op jit(solution)/shard_map/ppermute | solution.py:622
  44.8 1.1 %shard_map.75 = (f32[6,8,8,128]{3,2,1,0:T(8,128)S(1)}, f32[2,6,8,128]{3,2,1,0:T(8,128)S(1)}, f32[6,4,8,128]{3,2,1,0:T(8,128)S(1)}, f32[6,4,8,128]{3,2,1,0:T(8,12...) custom-call(f32[114,8,128]{2,1,0:T(8,128)S(1)} %shard_map.68.table_ref, ...), custom_call_target="tpu_custom_call" | custom-call | tf_op jit(solution)/shard_map/pallas_call | solution.py:603
  45.9 1.9 %collective-permute-start.8 = (f32[9,8,128]{2,1,0:T(8,128)S(1)}, f32[9,8,128]{2,1,0:T(8,128)S(1)}, u32[]{:S(2)}, u32[]{:S(2)}) collective-permute-start(f32[9,8,128]{2,1,0:T(8,128)S(1)} %get-tuple-element.38), channel_id=1, source_target_pairs={{0,12},{12,0},{24,36},{36,24},{48,60},{60,48},{72,84},{84,72},{96,... | collective-permute-start | bytes 110600 | tf_op jit(solution)/shard_map/ppermute | solution.py:623
  47.9 3.4 %collective-permute-start.9 = (f32[9,8,128]{2,1,0:T(8,128)S(1)}, f32[9,8,128]{2,1,0:T(8,128)S(1)}, u32[]{:S(2)}, u32[]{:S(2)}) collective-permute-start(f32[9,8,128]{2,1,0:T(8,128)S(1)} %get-tuple-element.39), channel_id=1, source_target_pairs={{0,756},{12,24},{24,12},{36,48},{48,36},{60,72},{72,60},{84,96},{9... | collective-permute-start | bytes 110600 | tf_op jit(solution)/shard_map/ppermute | solution.py:622
  51.2 0.7 %shard_map.76.part_ref = f32[6,4,8,128]{3,2,1,0:T(8,128)S(1)} custom-call(f32[114,8,128]{2,1,0:T(8,128)S(1)} %shard_map.68.table_ref, f32[6,4,8,128]{3,2,1,0:T(8,128)S(1)} %get-tuple-element.34.start_ref, f32[6,4,8,128]{3,2,1,0:T(8,128)S(1)} %get-tuple-element.35.c1_ref, f32[2,6,8,128]{3,2,1,0:T(8,128)S(1)} %get-tuple-element.33.h2_ref), custom_call_target="tpu_custom_call" | custom-call | tf_op jit(solution)/shard_map/pallas_call | solution.py:603
  51.9 0.0 collective-permute-done.8.ga
  51.9 4.5 %collective-permute-done.9.gb = f32[9,8,128]{2,1,0:T(8,128)S(1)} collective-permute-done((f32[9,8,128]{2,1,0:T(8,128)S(1)}, f32[9,8,128]{2,1,0:T(8,128)S(1)}, u32[]{:S(2)}, u32[]{:S(2)}) %collective-permute-start.9) | collective-permute-done | bytes 36896 | tf_op jit(solution)/shard_map/ppermute | solution.py:622
  56.4 1.4 %shard_map.77 = (f32[6,8,8,128]{3,2,1,0:T(8,128)}, f32[6,8,8,128]{3,2,1,0:T(8,128)}) custom-call(f32[114,8,128]{2,1,0:T(8,128)S(1)} %shard_map.68.table_ref, f32[6,8,8,128]{3,2,1,0:T(8,128)S(1)} %shard_map.74.t2_ref, f32[2,6,8,128]{3,2,1,0:T(8,128)S(1)} %get-tuple-element.33.h2_ref, f32[6,4,8,128]{3,2,1,0:T(8,128)S(1)} %get-tuple-element.34.start_ref, ...), custom_call_target="tpu_custom_call" | custom-call | tf_op jit(solution)/shard_map/pallas_call | solution.py:603
  (1 shorter events, 0.0 us)
Async XLA Ops:
  0.6 0.8 %copy-start.1 = (f32[8,8,128]{2,1,0:T(8,128)S(1)}, f32[8,8,128]{2,1,0:T(8,128)}, u32[]{:S(2)}) copy-start(f32[8,8,128]{2,1,0:T(8,128)} %dt_ref.13) | copy-start | bytes 98308
  0.6 0.9 %copy-start = (f32[6,8,8,128]{3,2,1,0:T(8,128)S(1)}, f32[6,8,8,128]{3,2,1,0:T(8,128)}, u32[]{:S(2)}) copy-start(f32[6,8,8,128]{3,2,1,0:T(8,128)} %q_ref.9) | copy-start | bytes 589828
  1.6 15.7 %copy-start.2 = (f32[3,6,6]{2,1,0:T(8,128)S(1)}, f32[3,6,6]{2,1,0:T(8,128)}, u32[]{:S(2)}) copy-start(f32[3,6,6]{2,1,0:T(8,128)} %a_ref.1) | copy-start | bytes 1300
  1.8 20.3 %collective-permute-start = (f32[12,8,128]{2,1,0:T(8,128)S(1)}, f32[12,8,128]{2,1,0:T(8,128)S(1)}, u32[]{:S(2)}, u32[]{:S(2)}) collective-permute-start(f32[12,8,128]{2,1,0:T(8,128)S(1)} %get-tuple-element.21), channel_id=1, source_target_pairs={{0,12},{12,0},{24,36},{36,24},{48,60},{60,48},{72,84},{84,72},{96,... | collective-permute-start | bytes 147464 | tf_op jit(solution)/shard_map/ppermute | solution.py:623
  3.7 18.4 %collective-permute-start.1 = (f32[12,8,128]{2,1,0:T(8,128)S(1)}, f32[12,8,128]{2,1,0:T(8,128)S(1)}, u32[]{:S(2)}, u32[]{:S(2)}) collective-permute-start(f32[12,8,128]{2,1,0:T(8,128)S(1)} %get-tuple-element.22), channel_id=1, source_target_pairs={{0,756},{12,24},{24,12},{36,48},{48,36},{60,72},{72,60},{84,96},{9... | collective-permute-start | bytes 147464 | tf_op jit(solution)/shard_map/ppermute | solution.py:622
  11.4 5.9 %copy-start.3 = (s32[1,2]{1,0:T(1,128)S(1)}, s32[1,2]{1,0:T(1,128)}, u32[]{:S(2)}) copy-start(s32[1,2]{1,0:T(1,128)} %type_ref.1) | copy-start | bytes 28
  11.4 5.9 %copy-start.4 = (s32[1,2]{1,0:T(1,128)S(1)}, s32[1,2]{1,0:T(1,128)}, u32[]{:S(2)}) copy-start(s32[1,2]{1,0:T(1,128)} %rot_ref.1) | copy-start | bytes 28
  11.4 6.7 %collective-permute-start.2 = (f32[7,8,128]{2,1,0:T(8,128)S(1)}, f32[7,8,128]{2,1,0:T(8,128)S(1)}, u32[]{:S(2)}, u32[]{:S(2)}) collective-permute-start(f32[7,8,128]{2,1,0:T(8,128)S(1)} %get-tuple-element.23), channel_id=1, source_target_pairs={{1,0},{2,1},{3,2},{4,3},{5,4},{6,5},{7,6},{8,7},{9,8},{10,9},{11,1... | collective-permute-start | bytes 86024 | tf_op jit(solution)/shard_map/ppermute | solution.py:634
  15.1 7.0 %collective-permute-start.3 = (f32[7,8,128]{2,1,0:T(8,128)S(1)}, f32[7,8,128]{2,1,0:T(8,128)S(1)}, u32[]{:S(2)}, u32[]{:S(2)}) collective-permute-start(f32[7,8,128]{2,1,0:T(8,128)S(1)} %get-tuple-element.24), channel_id=1, source_target_pairs={{0,1},{1,2},{2,3},{3,4},{4,5},{5,6},{6,7},{7,8},{8,9},{9,10},{10,1... | collective-permute-start | bytes 86024 | tf_op jit(solution)/shard_map/ppermute | solution.py:635
  22.5 6.0 %collective-permute-start.4 = (f32[15,8,128]{2,1,0:T(8,128)S(1)}, f32[15,8,128]{2,1,0:T(8,128)S(1)}, u32[]{:S(2)}, u32[]{:S(2)}) collective-permute-start(f32[15,8,128]{2,1,0:T(8,128)S(1)} %get-tuple-element.28), channel_id=1, source_target_pairs={{0,12},{12,0},{24,36},{36,24},{48,60},{60,48},{72,84},{84,72},{96,... | collective-permute-start | bytes 184328 | tf_op jit(solution)/shard_map/ppermute | solution.py:623
  24.5 8.9 %collective-permute-start.5 = (f32[15,8,128]{2,1,0:T(8,128)S(1)}, f32[15,8,128]{2,1,0:T(8,128)S(1)}, u32[]{:S(2)}, u32[]{:S(2)}) collective-permute-start(f32[15,8,128]{2,1,0:T(8,128)S(1)} %get-tuple-element.29), channel_id=1, source_target_pairs={{0,756},{12,24},{24,12},{36,48},{48,36},{60,72},{72,60},{84,96},{9... | collective-permute-start | bytes 184328 | tf_op jit(solution)/shard_map/ppermute | solution.py:622
  34.0 6.0 %collective-permute-start.6 = (f32[15,8,128]{2,1,0:T(8,128)S(1)}, f32[15,8,128]{2,1,0:T(8,128)S(1)}, u32[]{:S(2)}, u32[]{:S(2)}) collective-permute-start(f32[15,8,128]{2,1,0:T(8,128)S(1)} %get-tuple-element.31), channel_id=1, source_target_pairs={{0,12},{12,0},{24,36},{36,24},{48,60},{60,48},{72,84},{84,72},{96,... | collective-permute-start | bytes 184328 | tf_op jit(solution)/shard_map/ppermute | solution.py:623
  35.9 8.9 %collective-permute-start.7 = (f32[15,8,128]{2,1,0:T(8,128)S(1)}, f32[15,8,128]{2,1,0:T(8,128)S(1)}, u32[]{:S(2)}, u32[]{:S(2)}) collective-permute-start(f32[15,8,128]{2,1,0:T(8,128)S(1)} %get-tuple-element.32), channel_id=1, source_target_pairs={{0,756},{12,24},{24,12},{36,48},{48,36},{60,72},{72,60},{84,96},{9... | collective-permute-start | bytes 184328 | tf_op jit(solution)/shard_map/ppermute | solution.py:622
  45.9 6.0 %collective-permute-start.8 = (f32[9,8,128]{2,1,0:T(8,128)S(1)}, f32[9,8,128]{2,1,0:T(8,128)S(1)}, u32[]{:S(2)}, u32[]{:S(2)}) collective-permute-start(f32[9,8,128]{2,1,0:T(8,128)S(1)} %get-tuple-element.38), channel_id=1, source_target_pairs={{0,12},{12,0},{24,36},{36,24},{48,60},{60,48},{72,84},{84,72},{96,... | collective-permute-start | bytes 110600 | tf_op jit(solution)/shard_map/ppermute | solution.py:623
  47.9 8.6 %collective-permute-start.9 = (f32[9,8,128]{2,1,0:T(8,128)S(1)}, f32[9,8,128]{2,1,0:T(8,128)S(1)}, u32[]{:S(2)}, u32[]{:S(2)}) collective-permute-start(f32[9,8,128]{2,1,0:T(8,128)S(1)} %get-tuple-element.39), channel_id=1, source_target_pairs={{0,756},{12,24},{24,12},{36,48},{48,36},{60,72},{72,60},{84,96},{9... | collective-permute-start | bytes 110600 | tf_op jit(solution)/shard_map/ppermute | solution.py:622
where the time goes:
time: 58.2 us; the launch traced here: 57.8 us
  starting transfers between devices  31.3 us (54%)
  waiting for transfers between devices  18.1 us (31%)
  Pallas kernels  6.68 us (11%)
  local copies, waits for them, and re-layouts  0.91 us (2%)
  between operations  0.86 us (1%)
    ppermute x4, starting transfers between devices, exchange(): gb = lax.ppermute(mb, 'blk', link)  17.8 us
    ppermute x4, waiting for transfers between devices, exchange(): gb = lax.ppermute(mb, 'blk', link)  14.2 us
    ppermute x4, starting transfers between devices, exchange(): ga = lax.ppermute(ma, 'blk', chip)  7.68 us
    pallas_call x10, Pallas kernels, call(): pl.pallas_call(kernel, out_shape=[jax.ShapeDtypeStruct(shape, jnp.float32...  6.68 us
    ppermute x1, waiting for transfers between devices, cycle(): from_left = lax.ppermute(to_right, 'sub', ahead)  3.95 us
    ppermute x1, starting transfers between devices, cycle(): from_right = lax.ppermute(to_left, 'sub', back)  3.67 us
    ppermute x1, starting transfers between devices, cycle(): from_left = lax.ppermute(to_right, 'sub', ahead)  2.17 us
  transfers between devices with their start and end apart: 10, of which 4 were waited for; matrix products, arithmetic and copies ran while one was open for 0% of the time, Pallas kernels for 5%

commit v1 on v0

--- a/solution.py
+++ b/solution.py
@@ -402,9 +402,13 @@
     out_ref[...] = jnp.zeros_like(out_ref)
 
 
-def pack_kernel(prime_ref, q_ref, dt_ref, ends_ref, ma, mb, to_left, to_right):
-    rows = load(q_ref, 0, NI)
-    ends = pack_ends(rows)
+def pack_kernel(prime_ref, q_ref, dt_ref, ma, mb):
+    rows = [[q_ref[v, i] for v in range(NV)] for i in (0, 1, NI - 2, NI - 1)]
+    send_rows(ma, mb, 0, rows)
+
+
+def side_kernel(q_ref, dt_ref, ends_ref, to_left, to_right):
+    ends = pack_ends(load(q_ref, 0, NI))
     store_tiles(ends_ref, ends)
     r, lower = seg(), place() < HALO
     tiles = ends[0] + ends[1]
@@ -417,7 +421,6 @@
         x, y = tiles[2 * n], tiles[2 * n + 1]
         to_right[n] = jnp.where(lower, x, rotl(y, HALO))
         to_left[n] = jnp.where(lower, rotl(y, -HALO), x)
-    send_rows(ma, mb, 0, rows)
 
 
 def unpack(from_right, from_left):
@@ -625,10 +628,9 @@
 
     (table,) = call(table_kernel, (), (tiles_of(3 * NV * NV + 6),), (coupling, face_type, face_rot))
     (prime,) = call(prime_kernel, (), (tiles_of(114),))
-    ends, ma, mb, to_left, to_right = call(
-        pack_kernel,
-        (prime, flow_state, timestep),
-        (pair, tiles_of(2 * NV), tiles_of(2 * NV), tiles_of(NV + 1), tiles_of(NV + 1)),
+    ma, mb = call(pack_kernel, (prime, flow_state, timestep), (tiles_of(2 * NV), tiles_of(2 * NV)))
+    ends, to_left, to_right = call(
+        side_kernel, (flow_state, timestep), (pair, tiles_of(NV + 1), tiles_of(NV + 1))
     )
     ga, gb = exchange(ma, mb)
     from_right = lax.ppermute(to_left, "sub", back)

time: 58.2 us -> 58.3 us (level)
    pallas_call x10 -> x11, Pallas kernels: 6.68 us -> 6.7 us  [call(): pl.pallas_call(kernel, out_shape=[jax.ShapeDtypeStruct(shape, jnp.float32...]
where the time goes in v1:
time: 58.3 us; the launch traced here: 57.9 us
  starting transfers between devices  31.3 us (54%)
  waiting for transfers between devices  18.1 us (31%)
  Pallas kernels  6.7 us (11%)
  local copies, waits for them, and re-layouts  0.91 us (2%)
  between operations  0.87 us (1%)
    ppermute x4, starting transfers between devices, exchange(): gb = lax.ppermute(mb, 'blk', link)  17.8 us
    ppermute x4, waiting for transfers between devices, exchange(): gb = lax.ppermute(mb, 'blk', link)  14.2 us
    ppermute x4, starting transfers between devices, exchange(): ga = lax.ppermute(ma, 'blk', chip)  7.68 us
    pallas_call x11, Pallas kernels, call(): pl.pallas_call(kernel, out_shape=[jax.ShapeDtypeStruct(shape, jnp.float32...  6.7 us
    ppermute x1, waiting for transfers between devices, cycle(): from_left = lax.ppermute(to_right, 'sub', ahead)  3.95 us
    ppermute x1, starting transfers between devices, cycle(): from_right = lax.ppermute(to_left, 'sub', back)  3.67 us
    ppermute x1, starting transfers between devices, cycle(): from_left = lax.ppermute(to_right, 'sub', ahead)  2.17 us
  transfers between devices with their start and end apart: 10, of which 4 were waited for; matrix products, arithmetic and copies ran while one was open for 0% of the time, Pallas kernels for 5%

profile of v1, /device:TPU:512, one launch (start us, length us, event | category | flops | bytes accessed | tf_op | source)
XLA Modules:
  0.0 57.9 jit_solution(11179153278311922070)
XLA Ops:
  0.6 0.0 copy-start.1
  0.6 0.0 copy-start
  0.7 0.7 %copy-done.1 = f32[8,8,128]{2,1,0:T(8,128)S(1)} copy-done((f32[8,8,128]{2,1,0:T(8,128)S(1)}, f32[8,8,128]{2,1,0:T(8,128)}, u32[]{:S(2)}) %copy-start.1) | copy-done | bytes 32792
  1.4 0.2 copy-done
  1.6 1.9 %collective-permute-start = (f32[12,8,128]{2,1,0:T(8,128)S(1)}, f32[12,8,128]{2,1,0:T(8,128)S(1)}, u32[]{:S(2)}, u32[]{:S(2)}) collective-permute-start(f32[12,8,128]{2,1,0:T(8,128)S(1)} %get-tuple-element.21), channel_id=1, source_target_pairs={{0,12},{12,0},{24,36},{36,24},{48,60},{60,48},{72,84},{84,72},{96,... | collective-permute-start | bytes 147464 | tf_op jit(solution)/shard_map/ppermute | solution.py:626
  3.5 7.7 %collective-permute-start.1 = (f32[12,8,128]{2,1,0:T(8,128)S(1)}, f32[12,8,128]{2,1,0:T(8,128)S(1)}, u32[]{:S(2)}, u32[]{:S(2)}) collective-permute-start(f32[12,8,128]{2,1,0:T(8,128)S(1)} %get-tuple-element.22), channel_id=1, source_target_pairs={{0,756},{12,24},{24,12},{36,48},{48,36},{60,72},{72,60},{84,96},{9... | collective-permute-start | bytes 147464 | tf_op jit(solution)/shard_map/ppermute | solution.py:625
  11.2 0.0 copy-start.2
  11.2 0.2 shard_map.71
  11.4 0.0 copy-start.3
  11.4 0.0 copy-start.4
  11.4 3.7 %collective-permute-start.2 = (f32[7,8,128]{2,1,0:T(8,128)S(1)}, f32[7,8,128]{2,1,0:T(8,128)S(1)}, u32[]{:S(2)}, u32[]{:S(2)}) collective-permute-start(f32[7,8,128]{2,1,0:T(8,128)S(1)} %get-tuple-element.23), channel_id=1, source_target_pairs={{1,0},{2,1},{3,2},{4,3},{5,4},{6,5},{7,6},{8,7},{9,8},{10,9},{11,1... | collective-permute-start | bytes 86024 | tf_op jit(solution)/shard_map/ppermute | solution.py:636
  15.1 2.2 %collective-permute-start.3 = (f32[7,8,128]{2,1,0:T(8,128)S(1)}, f32[7,8,128]{2,1,0:T(8,128)S(1)}, u32[]{:S(2)}, u32[]{:S(2)}) collective-permute-start(f32[7,8,128]{2,1,0:T(8,128)S(1)} %get-tuple-element.24), channel_id=1, source_target_pairs={{0,1},{1,2},{2,3},{3,4},{4,5},{5,6},{6,7},{7,8},{8,9},{9,10},{10,1... | collective-permute-start | bytes 86024 | tf_op jit(solution)/shard_map/ppermute | solution.py:637
  17.3 0.0 copy-done.2
  17.3 0.0 copy-done.3
  17.3 0.0 copy-done.4
  17.3 0.8 %shard_map.68.table_ref = f32[114,8,128]{2,1,0:T(8,128)S(1)} custom-call(f32[3,6,6]{2,1,0:T(8,128)S(1)} %copy-done.2, s32[1,2]{1,0:T(1,128)S(1)} %copy-done.3, s32[1,2]{1,0:T(1,128)S(1)} %copy-done.4), custom_call_target="tpu_custom_call" | custom-call | tf_op jit(solution)/shard_map/pallas_call | solution.py:606
  18.1 0.0 collective-permute-done.2.from_right
  18.1 3.9 %collective-permute-done.3.from_left = f32[7,8,128]{2,1,0:T(8,128)S(1)} collective-permute-done((f32[7,8,128]{2,1,0:T(8,128)S(1)}, f32[7,8,128]{2,1,0:T(8,128)S(1)}, u32[]{:S(2)}, u32[]{:S(2)}) %collective-permute-start.3) | collective-permute-done | bytes 28704 | tf_op jit(solution)/shard_map/ppermute | solution.py:637
  22.1 0.0 collective-permute-done.ga
  22.1 0.0 collective-permute-done.1.gb
  22.1 0.5 shard_map.72
  22.6 1.9 %collective-permute-start.4 = (f32[15,8,128]{2,1,0:T(8,128)S(1)}, f32[15,8,128]{2,1,0:T(8,128)S(1)}, u32[]{:S(2)}, u32[]{:S(2)}) collective-permute-start(f32[15,8,128]{2,1,0:T(8,128)S(1)} %get-tuple-element.28), channel_id=1, source_target_pairs={{0,12},{12,0},{24,36},{36,24},{48,60},{60,48},{72,84},{84,72},{96,... | collective-permute-start | bytes 184328 | tf_op jit(solution)/shard_map/ppermute | solution.py:626
  24.5 3.4 %collective-permute-start.5 = (f32[15,8,128]{2,1,0:T(8,128)S(1)}, f32[15,8,128]{2,1,0:T(8,128)S(1)}, u32[]{:S(2)}, u32[]{:S(2)}) collective-permute-start(f32[15,8,128]{2,1,0:T(8,128)S(1)} %get-tuple-element.29), channel_id=1, source_target_pairs={{0,756},{12,24},{24,12},{36,48},{48,36},{60,72},{72,60},{84,96},{9... | collective-permute-start | bytes 184328 | tf_op jit(solution)/shard_map/ppermute | solution.py:625
  27.9 0.7 %shard_map.73.t1_ref = f32[6,8,8,128]{3,2,1,0:T(8,128)S(1)} custom-call(f32[114,8,128]{2,1,0:T(8,128)S(1)} %shard_map.68.table_ref, f32[6,8,8,128]{3,2,1,0:T(8,128)S(1)} %copy-done, f32[8,8,128]{2,1,0:T(8,128)S(1)} %copy-done.1, f32[12,8,128]{2,1,0:T(8,128)S(1)} %collective-permute-done.ga, f32[12,8,128]{2,1,0:T(8,128)S(1)} %collective-permute-done.1.gb, ...), custom_call_target="tpu_custom_call" | custom-call | tf_op jit(solution)/shard_map/pallas_call | solution.py:606
  28.5 0.0 collective-permute-done.4.ga
  28.6 4.8 %collective-permute-done.5.gb = f32[15,8,128]{2,1,0:T(8,128)S(1)} collective-permute-done((f32[15,8,128]{2,1,0:T(8,128)S(1)}, f32[15,8,128]{2,1,0:T(8,128)S(1)}, u32[]{:S(2)}, u32[]{:S(2)}) %collective-permute-start.5) | collective-permute-done | bytes 61472 | tf_op jit(solution)/shard_map/ppermute | solution.py:625
  33.4 0.7 %shard_map.74 = (f32[2,6,8,128]{3,2,1,0:T(8,128)S(1)}, f32[15,8,128]{2,1,0:T(8,128)S(1)}, f32[15,8,128]{2,1,0:T(8,128)S(1)}) custom-call(f32[114,8,128]{2,1,0:T(8,128)S(1)} %shard_map.68.table_ref, f32[6,8,8,128]{3,2,1,0:T(8,128)S(1)} %copy-done, f32[6,8,8,128]{3,2,1,0:T(8,128)S(1)} %shard_map.73.t1_ref, f32[2,6,8,128]{3,2,1,0:T(8,128)S(1)} %get-tuple-element.25.h0_ref, ...), custom_call_target="tpu_custom_call" | custom-call | tf_op jit(solution)/shard_map/pallas_call | solution.py:606
  34.0 1.9 %collective-permute-start.6 = (f32[15,8,128]{2,1,0:T(8,128)S(1)}, f32[15,8,128]{2,1,0:T(8,128)S(1)}, u32[]{:S(2)}, u32[]{:S(2)}) collective-permute-start(f32[15,8,128]{2,1,0:T(8,128)S(1)} %get-tuple-element.31), channel_id=1, source_target_pairs={{0,12},{12,0},{24,36},{36,24},{48,60},{60,48},{72,84},{84,72},{96,... | collective-permute-start | bytes 184328 | tf_op jit(solution)/shard_map/ppermute | solution.py:626
  36.0 3.4 %collective-permute-start.7 = (f32[15,8,128]{2,1,0:T(8,128)S(1)}, f32[15,8,128]{2,1,0:T(8,128)S(1)}, u32[]{:S(2)}, u32[]{:S(2)}) collective-permute-start(f32[15,8,128]{2,1,0:T(8,128)S(1)} %get-tuple-element.32), channel_id=1, source_target_pairs={{0,756},{12,24},{24,12},{36,48},{48,36},{60,72},{72,60},{84,96},{9... | collective-permute-start | bytes 184328 | tf_op jit(solution)/shard_map/ppermute | solution.py:625
  39.3 0.7 %shard_map.75.t2_ref = f32[6,8,8,128]{3,2,1,0:T(8,128)S(1)} custom-call(f32[114,8,128]{2,1,0:T(8,128)S(1)} %shard_map.68.table_ref, f32[6,8,8,128]{3,2,1,0:T(8,128)S(1)} %copy-done, f32[6,8,8,128]{3,2,1,0:T(8,128)S(1)} %shard_map.73.t1_ref, f32[2,6,8,128]{3,2,1,0:T(8,128)S(1)} %get-tuple-element.30.h1_ref, f32[8,8,128]{2,1,0:T(8,128)S(1)} %copy-done.1, ...), custom_call_target="tpu_custom_call" | custom-call | tf_op jit(solution)/shard_map/pallas_call | solution.py:606
  40.0 0.0 collective-permute-done.6.ga
  40.0 4.8 %collective-permute-done.7.gb = f32[15,8,128]{2,1,0:T(8,128)S(1)} collective-permute-done((f32[15,8,128]{2,1,0:T(8,128)S(1)}, f32[15,8,128]{2,1,0:T(8,128)S(1)}, u32[]{:S(2)}, u32[]{:S(2)}) %collective-permute-start.7) | collective-permute-done | bytes 61472 | tf_op jit(solution)/shard_map/ppermute | solution.py:625
  44.8 1.1 %shard_map.76 = (f32[6,8,8,128]{3,2,1,0:T(8,128)S(1)}, f32[2,6,8,128]{3,2,1,0:T(8,128)S(1)}, f32[6,4,8,128]{3,2,1,0:T(8,128)S(1)}, f32[6,4,8,128]{3,2,1,0:T(8,12...) custom-call(f32[114,8,128]{2,1,0:T(8,128)S(1)} %shard_map.68.table_ref, ...), custom_call_target="tpu_custom_call" | custom-call | tf_op jit(solution)/shard_map/pallas_call | solution.py:606
  46.0 1.9 %collective-permute-start.8 = (f32[9,8,128]{2,1,0:T(8,128)S(1)}, f32[9,8,128]{2,1,0:T(8,128)S(1)}, u32[]{:S(2)}, u32[]{:S(2)}) collective-permute-start(f32[9,8,128]{2,1,0:T(8,128)S(1)} %get-tuple-element.38), channel_id=1, source_target_pairs={{0,12},{12,0},{24,36},{36,24},{48,60},{60,48},{72,84},{84,72},{96,... | collective-permute-start | bytes 110600 | tf_op jit(solution)/shard_map/ppermute | solution.py:626
  47.9 3.4 %collective-permute-start.9 = (f32[9,8,128]{2,1,0:T(8,128)S(1)}, f32[9,8,128]{2,1,0:T(8,128)S(1)}, u32[]{:S(2)}, u32[]{:S(2)}) collective-permute-start(f32[9,8,128]{2,1,0:T(8,128)S(1)} %get-tuple-element.39), channel_id=1, source_target_pairs={{0,756},{12,24},{24,12},{36,48},{48,36},{60,72},{72,60},{84,96},{9... | collective-permute-start | bytes 110600 | tf_op jit(solution)/shard_map/ppermute | solution.py:625
  51.2 0.7 %shard_map.77.part_ref = f32[6,4,8,128]{3,2,1,0:T(8,128)S(1)} custom-call(f32[114,8,128]{2,1,0:T(8,128)S(1)} %shard_map.68.table_ref, f32[6,4,8,128]{3,2,1,0:T(8,128)S(1)} %get-tuple-element.34.start_ref, f32[6,4,8,128]{3,2,1,0:T(8,128)S(1)} %get-tuple-element.35.c1_ref, f32[2,6,8,128]{3,2,1,0:T(8,128)S(1)} %get-tuple-element.33.h2_ref), custom_call_target="tpu_custom_call" | custom-call | tf_op jit(solution)/shard_map/pallas_call | solution.py:606
  51.9 0.0 collective-permute-done.8.ga
  51.9 4.5 %collective-permute-done.9.gb = f32[9,8,128]{2,1,0:T(8,128)S(1)} collective-permute-done((f32[9,8,128]{2,1,0:T(8,128)S(1)}, f32[9,8,128]{2,1,0:T(8,128)S(1)}, u32[]{:S(2)}, u32[]{:S(2)}) %collective-permute-start.9) | collective-permute-done | bytes 36896 | tf_op jit(solution)/shard_map/ppermute | solution.py:625
  56.5 1.4 %shard_map.78 = (f32[6,8,8,128]{3,2,1,0:T(8,128)}, f32[6,8,8,128]{3,2,1,0:T(8,128)}) custom-call(f32[114,8,128]{2,1,0:T(8,128)S(1)} %shard_map.68.table_ref, f32[6,8,8,128]{3,2,1,0:T(8,128)S(1)} %shard_map.75.t2_ref, f32[2,6,8,128]{3,2,1,0:T(8,128)S(1)} %get-tuple-element.33.h2_ref, f32[6,4,8,128]{3,2,1,0:T(8,128)S(1)} %get-tuple-element.34.start_ref, ...), custom_call_target="tpu_custom_call" | custom-call | tf_op jit(solution)/shard_map/pallas_call | solution.py:606
  (2 shorter events, 0.0 us)
Async XLA Ops:
  0.6 0.8 %copy-start.1 = (f32[8,8,128]{2,1,0:T(8,128)S(1)}, f32[8,8,128]{2,1,0:T(8,128)}, u32[]{:S(2)}) copy-start(f32[8,8,128]{2,1,0:T(8,128)} %dt_ref.15) | copy-start | bytes 98308
  0.6 0.9 %copy-start = (f32[6,8,8,128]{3,2,1,0:T(8,128)S(1)}, f32[6,8,8,128]{3,2,1,0:T(8,128)}, u32[]{:S(2)}) copy-start(f32[6,8,8,128]{3,2,1,0:T(8,128)} %q_ref.11) | copy-start | bytes 589828
  1.6 20.5 %collective-permute-start = (f32[12,8,128]{2,1,0:T(8,128)S(1)}, f32[12,8,128]{2,1,0:T(8,128)S(1)}, u32[]{:S(2)}, u32[]{:S(2)}) collective-permute-start(f32[12,8,128]{2,1,0:T(8,128)S(1)} %get-tuple-element.21), channel_id=1, source_target_pairs={{0,12},{12,0},{24,36},{36,24},{48,60},{60,48},{72,84},{84,72},{96,... | collective-permute-start | bytes 147464 | tf_op jit(solution)/shard_map/ppermute | solution.py:626
  3.5 18.6 %collective-permute-start.1 = (f32[12,8,128]{2,1,0:T(8,128)S(1)}, f32[12,8,128]{2,1,0:T(8,128)S(1)}, u32[]{:S(2)}, u32[]{:S(2)}) collective-permute-start(f32[12,8,128]{2,1,0:T(8,128)S(1)} %get-tuple-element.22), channel_id=1, source_target_pairs={{0,756},{12,24},{24,12},{36,48},{48,36},{60,72},{72,60},{84,96},{9... | collective-permute-start | bytes 147464 | tf_op jit(solution)/shard_map/ppermute | solution.py:625
  11.2 6.1 %copy-start.2 = (f32[3,6,6]{2,1,0:T(8,128)S(1)}, f32[3,6,6]{2,1,0:T(8,128)}, u32[]{:S(2)}) copy-start(f32[3,6,6]{2,1,0:T(8,128)} %a_ref.1) | copy-start | bytes 1300
  11.4 5.9 %copy-start.3 = (s32[1,2]{1,0:T(1,128)S(1)}, s32[1,2]{1,0:T(1,128)}, u32[]{:S(2)}) copy-start(s32[1,2]{1,0:T(1,128)} %type_ref.1) | copy-start | bytes 28
  11.4 5.9 %copy-start.4 = (s32[1,2]{1,0:T(1,128)S(1)}, s32[1,2]{1,0:T(1,128)}, u32[]{:S(2)}) copy-start(s32[1,2]{1,0:T(1,128)} %rot_ref.1) | copy-start | bytes 28
  11.4 6.7 %collective-permute-start.2 = (f32[7,8,128]{2,1,0:T(8,128)S(1)}, f32[7,8,128]{2,1,0:T(8,128)S(1)}, u32[]{:S(2)}, u32[]{:S(2)}) collective-permute-start(f32[7,8,128]{2,1,0:T(8,128)S(1)} %get-tuple-element.23), channel_id=1, source_target_pairs={{1,0},{2,1},{3,2},{4,3},{5,4},{6,5},{7,6},{8,7},{9,8},{10,9},{11,1... | collective-permute-start | bytes 86024 | tf_op jit(solution)/shard_map/ppermute | solution.py:636
  15.1 7.0 %collective-permute-start.3 = (f32[7,8,128]{2,1,0:T(8,128)S(1)}, f32[7,8,128]{2,1,0:T(8,128)S(1)}, u32[]{:S(2)}, u32[]{:S(2)}) collective-permute-start(f32[7,8,128]{2,1,0:T(8,128)S(1)} %get-tuple-element.24), channel_id=1, source_target_pairs={{0,1},{1,2},{2,3},{3,4},{4,5},{5,6},{6,7},{7,8},{8,9},{9,10},{10,1... | collective-permute-start | bytes 86024 | tf_op jit(solution)/shard_map/ppermute | solution.py:637
  22.6 6.0 %collective-permute-start.4 = (f32[15,8,128]{2,1,0:T(8,128)S(1)}, f32[15,8,128]{2,1,0:T(8,128)S(1)}, u32[]{:S(2)}, u32[]{:S(2)}) collective-permute-start(f32[15,8,128]{2,1,0:T(8,128)S(1)} %get-tuple-element.28), channel_id=1, source_target_pairs={{0,12},{12,0},{24,36},{36,24},{48,60},{60,48},{72,84},{84,72},{96,... | collective-permute-start | bytes 184328 | tf_op jit(solution)/shard_map/ppermute | solution.py:626
  24.5 8.9 %collective-permute-start.5 = (f32[15,8,128]{2,1,0:T(8,128)S(1)}, f32[15,8,128]{2,1,0:T(8,128)S(1)}, u32[]{:S(2)}, u32[]{:S(2)}) collective-permute-start(f32[15,8,128]{2,1,0:T(8,128)S(1)} %get-tuple-element.29), channel_id=1, source_target_pairs={{0,756},{12,24},{24,12},{36,48},{48,36},{60,72},{72,60},{84,96},{9... | collective-permute-start | bytes 184328 | tf_op jit(solution)/shard_map/ppermute | solution.py:625
  34.0 6.0 %collective-permute-start.6 = (f32[15,8,128]{2,1,0:T(8,128)S(1)}, f32[15,8,128]{2,1,0:T(8,128)S(1)}, u32[]{:S(2)}, u32[]{:S(2)}) collective-permute-start(f32[15,8,128]{2,1,0:T(8,128)S(1)} %get-tuple-element.31), channel_id=1, source_target_pairs={{0,12},{12,0},{24,36},{36,24},{48,60},{60,48},{72,84},{84,72},{96,... | collective-permute-start | bytes 184328 | tf_op jit(solution)/shard_map/ppermute | solution.py:626
  36.0 8.9 %collective-permute-start.7 = (f32[15,8,128]{2,1,0:T(8,128)S(1)}, f32[15,8,128]{2,1,0:T(8,128)S(1)}, u32[]{:S(2)}, u32[]{:S(2)}) collective-permute-start(f32[15,8,128]{2,1,0:T(8,128)S(1)} %get-tuple-element.32), channel_id=1, source_target_pairs={{0,756},{12,24},{24,12},{36,48},{48,36},{60,72},{72,60},{84,96},{9... | collective-permute-start | bytes 184328 | tf_op jit(solution)/shard_map/ppermute | solution.py:625
  46.0 6.0 %collective-permute-start.8 = (f32[9,8,128]{2,1,0:T(8,128)S(1)}, f32[9,8,128]{2,1,0:T(8,128)S(1)}, u32[]{:S(2)}, u32[]{:S(2)}) collective-permute-start(f32[9,8,128]{2,1,0:T(8,128)S(1)} %get-tuple-element.38), channel_id=1, source_target_pairs={{0,12},{12,0},{24,36},{36,24},{48,60},{60,48},{72,84},{84,72},{96,... | collective-permute-start | bytes 110600 | tf_op jit(solution)/shard_map/ppermute | solution.py:626
  47.9 8.6 %collective-permute-start.9 = (f32[9,8,128]{2,1,0:T(8,128)S(1)}, f32[9,8,128]{2,1,0:T(8,128)S(1)}, u32[]{:S(2)}, u32[]{:S(2)}) collective-permute-start(f32[9,8,128]{2,1,0:T(8,128)S(1)} %get-tuple-element.39), channel_id=1, source_target_pairs={{0,756},{12,24},{24,12},{36,48},{48,36},{60,72},{72,60},{84,96},{9... | collective-permute-start | bytes 110600 | tf_op jit(solution)/shard_map/ppermute | solution.py:625
